TPU v7x, 32 devices: a whole 2x2x4 slice. The times are simulated.
32 devices in a mesh: batch: 8 (over y, x, core), cols: 4 (over z).
Axes of the slice: x: 2, y: 2, z: 4, core: 2. Of those that a mesh axis runs over, the one named last changes fastest.
Arguments:
- grad_up: float32 [8, 1024, 4096], P('batch', None, 'cols'), may hold values from -0.875 to 0.875
- grad_down: float32 [8, 4096, 1024], P('batch', 'cols'), may hold values from -0.875 to 0.875
- grad_query: float32 [8, 1024, 1024], P('batch', None, 'cols'), may hold values from -0.875 to 0.875
- grad_key: float32 [8, 1024, 1024], P('batch', None, 'cols'), may hold values from -0.875 to 0.875
- grad_value: float32 [8, 1024, 1024], P('batch', None, 'cols'), may hold values from -0.875 to 0.875
- grad_mixed: float32 [8, 1024, 1024], P('batch', 'cols'), may hold values from -0.875 to 0.875
- grad_norm: float32 [8, 1024], P('batch'), may hold values from -8 to 8
- grad_bias: float32 [8, 1024], P('batch'), may hold values from -8 to 8
- weight_up: float32 [1024, 4096], P('batch', 'cols'), may hold values from -0.25 to 0.25
- weight_down: float32 [4096, 1024], P('cols', 'batch'), may hold values from -0.125 to 0.125
- weight_query: float32 [1024, 1024], P('batch', 'cols'), may hold values from -0.25 to 0.25
- weight_key: float32 [1024, 1024], P('batch', 'cols'), may hold values from -0.25 to 0.25
- weight_value: float32 [1024, 1024], P('batch', 'cols'), may hold values from -0.25 to 0.25
- weight_mixed: float32 [1024, 1024], P('cols', 'batch'), may hold values from -0.25 to 0.25
- weight_norm: float32 [1024], P('batch'), may hold values from 0.25 to 1.75
- weight_bias: float32 [1024], P('batch'), may hold values from -3 to 3
Outputs:
- copy_up: bfloat16 [1024, 4096], P(None, 'cols')
- copy_down: bfloat16 [4096, 1024], P('cols')
- copy_query: bfloat16 [1024, 1024], P(None, 'cols')
- copy_key: bfloat16 [1024, 1024], P(None, 'cols')
- copy_value: bfloat16 [1024, 1024], P(None, 'cols')
- copy_mixed: bfloat16 [1024, 1024], P('cols')
- copy_norm: bfloat16 [1024], replicated
- copy_bias: bfloat16 [1024], replicated
- new_up: float32 [1024, 4096], P('batch', 'cols')
- new_down: float32 [4096, 1024], P('cols', 'batch')
- new_query: float32 [1024, 1024], P('batch', 'cols')
- new_key: float32 [1024, 1024], P('batch', 'cols')
- new_value: float32 [1024, 1024], P('batch', 'cols')
- new_mixed: float32 [1024, 1024], P('cols', 'batch')
- new_norm: float32 [1024], P('batch')
- new_bias: float32 [1024], P('batch')
All inputs are finite; a program needn't handle non-finite values.
Results may differ from a plain program's by a relative error of at most 0.0075.
Values may be sent and summed in bfloat16 or wider, within the bound.
A program may use at most 64 MiB of HBM per device.

v0:
```python
import jax
import jax.numpy as jnp
from jax import lax
from jax.sharding import PartitionSpec as P

learn_rate = 0.3


def local(
    grad_up,
    grad_down,
    grad_query,
    grad_key,
    grad_value,
    grad_mixed,
    grad_norm,
    grad_bias,
    weight_up,
    weight_down,
    weight_query,
    weight_key,
    weight_value,
    weight_mixed,
    weight_norm,
    weight_bias,
):
    mean_up, mean_down, mean_query, mean_key, mean_value, mean_mixed = (
        lax.psum_scatter(
            grad_up[0].astype(jnp.float32).astype(jnp.bfloat16),
            "batch",
            scatter_dimension=0,
            tiled=True,
        ).astype(jnp.float32),
        lax.psum_scatter(
            grad_down[0].astype(jnp.float32).astype(jnp.bfloat16),
            "batch",
            scatter_dimension=1,
            tiled=True,
        ).astype(jnp.float32),
        lax.psum_scatter(
            grad_query[0].astype(jnp.float32).astype(jnp.bfloat16),
            "batch",
            scatter_dimension=0,
            tiled=True,
        ).astype(jnp.float32),
        lax.psum_scatter(
            grad_key[0].astype(jnp.float32).astype(jnp.bfloat16),
            "batch",
            scatter_dimension=0,
            tiled=True,
        ).astype(jnp.float32),
        lax.psum_scatter(
            grad_value[0].astype(jnp.float32).astype(jnp.bfloat16),
            "batch",
            scatter_dimension=0,
            tiled=True,
        ).astype(jnp.float32),
        lax.psum_scatter(
            grad_mixed[0].astype(jnp.float32).astype(jnp.bfloat16),
            "batch",
            scatter_dimension=1,
            tiled=True,
        ).astype(jnp.float32),
    )
    whole_norm, whole_bias = lax.psum(
        (grad_norm[0].astype(jnp.float32), grad_bias[0].astype(jnp.float32)), "batch"
    )
    place = lax.axis_index("batch")
    mean_norm = lax.dynamic_slice_in_dim(
        whole_norm, place * weight_norm.shape[0], weight_norm.shape[0]
    )
    mean_bias = lax.dynamic_slice_in_dim(
        whole_bias, place * weight_bias.shape[0], weight_bias.shape[0]
    )
    mean_rate = lax.axis_size("batch") ** (-0.5)
    mean_up = mean_up * mean_rate
    mean_down = mean_down * mean_rate
    mean_query = mean_query * mean_rate
    mean_key = mean_key * mean_rate
    mean_value = mean_value * mean_rate
    mean_mixed = mean_mixed * mean_rate
    mean_norm = mean_norm * mean_rate
    mean_bias = mean_bias * mean_rate
    (
        own_up,
        own_down,
        own_query,
        own_key,
        own_value,
        own_mixed,
        slope_up_norm,
        slope_down_norm,
        slope_query_norm,
        slope_key_norm,
        slope_value_norm,
        slope_mixed_norm,
    ) = lax.psum(
        (
            jnp.sum(weight_up * weight_up, axis=1, keepdims=True),
            jnp.sum(weight_down * weight_down, axis=0, keepdims=True),
            jnp.sum(weight_query * weight_query, axis=1, keepdims=True),
            jnp.sum(weight_key * weight_key, axis=1, keepdims=True),
            jnp.sum(weight_value * weight_value, axis=1, keepdims=True),
            jnp.sum(weight_mixed * weight_mixed, axis=0, keepdims=True),
            jnp.sum(mean_up * mean_up, axis=1, keepdims=True),
            jnp.sum(mean_down * mean_down, axis=0, keepdims=True),
            jnp.sum(mean_query * mean_query, axis=1, keepdims=True),
            jnp.sum(mean_key * mean_key, axis=1, keepdims=True),
            jnp.sum(mean_value * mean_value, axis=1, keepdims=True),
            jnp.sum(mean_mixed * mean_mixed, axis=0, keepdims=True),
        ),
        "cols",
    )
    mean_up = mean_up * (jnp.sqrt(own_up) * lax.rsqrt(slope_up_norm + 1e-06))
    mean_down = mean_down * (jnp.sqrt(own_down) * lax.rsqrt(slope_down_norm + 1e-06))
    mean_query = mean_query * (jnp.sqrt(own_query) * lax.rsqrt(slope_query_norm + 1e-06))
    mean_key = mean_key * (jnp.sqrt(own_key) * lax.rsqrt(slope_key_norm + 1e-06))
    mean_value = mean_value * (jnp.sqrt(own_value) * lax.rsqrt(slope_value_norm + 1e-06))
    mean_mixed = mean_mixed * (jnp.sqrt(own_mixed) * lax.rsqrt(slope_mixed_norm + 1e-06))
    new_up = weight_up - learn_rate * mean_up
    new_down = weight_down - learn_rate * mean_down
    new_query = weight_query - learn_rate * mean_query
    new_key = weight_key - learn_rate * mean_key
    new_value = weight_value - learn_rate * mean_value
    new_mixed = weight_mixed - learn_rate * mean_mixed
    new_norm = weight_norm - learn_rate * mean_norm
    new_bias = weight_bias - learn_rate * mean_bias
    copy_up, copy_down, copy_query, copy_key, copy_value, copy_mixed, copy_norm, copy_bias = (
        lax.all_gather(new_up.astype(jnp.bfloat16), "batch", axis=0, tiled=True),
        lax.all_gather(new_down.astype(jnp.bfloat16), "batch", axis=1, tiled=True),
        lax.all_gather(new_query.astype(jnp.bfloat16), "batch", axis=0, tiled=True),
        lax.all_gather(new_key.astype(jnp.bfloat16), "batch", axis=0, tiled=True),
        lax.all_gather(new_value.astype(jnp.bfloat16), "batch", axis=0, tiled=True),
        lax.all_gather(new_mixed.astype(jnp.bfloat16), "batch", axis=1, tiled=True),
        lax.all_gather(new_norm.astype(jnp.bfloat16), "batch", axis=0, tiled=True),
        lax.all_gather(new_bias.astype(jnp.bfloat16), "batch", axis=0, tiled=True),
    )
    return (
        copy_up,
        copy_down,
        copy_query,
        copy_key,
        copy_value,
        copy_mixed,
        copy_norm,
        copy_bias,
        new_up,
        new_down,
        new_query,
        new_key,
        new_value,
        new_mixed,
        new_norm,
        new_bias,
    )


def solution(mesh):
    in_specs = (
        P("batch", None, "cols"),
        P("batch", "cols", None),
        P("batch", None, "cols"),
        P("batch", None, "cols"),
        P("batch", None, "cols"),
        P("batch", "cols", None),
        P("batch", None),
        P("batch", None),
        P("batch", "cols"),
        P("cols", "batch"),
        P("batch", "cols"),
        P("batch", "cols"),
        P("batch", "cols"),
        P("cols", "batch"),
        P("batch"),
        P("batch"),
    )
    out_specs = (
        P(None, "cols"),
        P("cols", None),
        P(None, "cols"),
        P(None, "cols"),
        P(None, "cols"),
        P("cols", None),
        P(),
        P(),
        P("batch", "cols"),
        P("cols", "batch"),
        P("batch", "cols"),
        P("batch", "cols"),
        P("batch", "cols"),
        P("cols", "batch"),
        P("batch"),
        P("batch"),
    )
    return jax.shard_map(local, mesh=mesh, in_specs=in_specs, out_specs=out_specs, check_vma=False)
```

profile of v0, /device:TPU:0, one launch (start us, length us, event | category | flops | bytes accessed | tf_op | source)
XLA Modules:
  0.0 357.3 jit_solution(12971309623666984505)
XLA Ops:
  7.2 1.4 convert_bitcast_fusion.2
  8.6 1.0 copy.34
  9.7 0.8 convert_bitcast_fusion.5
  10.7 0.8 convert_bitcast_fusion.4
  11.6 0.8 convert_bitcast_fusion.3
  12.5 2.5 convert_bitcast_fusion
  15.0 2.6 copy.32
  17.7 3.8 %convert_bitcast_fusion.1 = bf16[1024,1024]{1,0:T(8,128)(2,1)} fusion(f32[1,1024,1024]{2,1,0:T(8,128)} %param.16), kind=kLoop, calls=%fused_computation.1 | loop fusion | flops 1048576 | bytes 6291456 | tf_op jit(solution)/shard_map/convert_element_type | solution.py:29
  23.1 25.5 %reduce-scatter.21.cloned.1.call-done = bf16[128,256]{1,0:T(8,128)(2,1)} async-done(((bf16[1024,256]{1,0:T(8,128)(2,1)}), bf16[128,256]{1,0:T(8,128)(2,1)}) %reduce-scatter.21.cloned.1.call-update) | async-done | bytes 65552
  48.6 0.9 copy.35
  49.6 36.8 %reduce-scatter.13.cloned.1.call-done = bf16[128,256]{1,0:T(8,128)(2,1)} async-done(((bf16[1024,256]{1,0:T(8,128)(2,1)}), bf16[128,256]{1,0:T(8,128)(2,1)}) %reduce-scatter.13.cloned.1.call-update) | async-done | bytes 65552 | tf_op jit(solution)/shard_map/reduce_scatter | solution.py:40
  86.4 0.9 fusion.9
  87.4 36.9 %reduce-scatter.15.cloned.1.call-done = bf16[128,256]{1,0:T(8,128)(2,1)} async-done(((bf16[1024,256]{1,0:T(8,128)(2,1)}), bf16[128,256]{1,0:T(8,128)(2,1)}) %reduce-scatter.15.cloned.1.call-update) | async-done | bytes 65552 | tf_op jit(solution)/shard_map/reduce_scatter | solution.py:46
  124.3 0.9 fusion.13
  125.2 36.7 %reduce-scatter.17.cloned.1.call-done = bf16[128,256]{1,0:T(8,128)(2,1)} async-done(((bf16[1024,256]{1,0:T(8,128)(2,1)}), bf16[128,256]{1,0:T(8,128)(2,1)}) %reduce-scatter.17.cloned.1.call-update) | async-done | bytes 65552 | tf_op jit(solution)/shard_map/reduce_scatter | solution.py:52
  162.0 0.9 fusion.17
  162.9 43.7 %reduce-scatter.19.cloned.1.call-done = bf16[128,1024]{1,0:T(8,128)(2,1)} async-done(((bf16[1024,1024]{1,0:T(8,128)(2,1)}), bf16[128,1024]{1,0:T(8,128)(2,1)}) %reduce-scatter.19.cloned.1.call-update) | async-done | bytes 262160
  206.6 1.1 copy.33
  207.9 43.3 %reduce-scatter.11.cloned.1.call-done = bf16[128,1024]{1,0:T(8,128)(2,1)} async-done(((bf16[1024,1024]{1,0:T(8,128)(2,1)}), bf16[128,1024]{1,0:T(8,128)(2,1)}) %reduce-scatter.11.cloned.1.call-update) | async-done | bytes 262160 | tf_op jit(solution)/shard_map/reduce_scatter | solution.py:28
  251.3 1.1 fusion.1
  252.4 11.8 %all-reduce.1 = (f32[128,1]{0,1:T(1,128)S(1)}, f32[128,1]{0,1:T(1,128)S(1)}, f32[1,128]{1,0:T(1,128)S(1)}, f32[1,128]{1,0:T(1,128)S(1)}, f32[128,1]{0,1:T(1,128)...) all-reduce(f32[128,1]{0,1:T(1,128)S(1)} %bitcast.65, ...), channel_id=1, replica_groups=mesh['batch'=8,'cols'=4] {'cols'}, use_global_device_ids=true, to_apply=%region_4.0 | all-reduce | flops 1536 | bytes 12288 | tf_op jit(solution)/shard_map/psum | solution.py:97
  264.2 2.0 fusion.34
  266.3 1.0 fusion.32
  267.3 12.0 %all-reduce = (f32[1024]{0:T(1024)S(1)}, f32[1024]{0:T(1024)S(1)}) all-reduce(f32[1024]{0:T(1024)S(1)} %bitcast.52, f32[1024]{0:T(1024)S(1)} %bitcast.53), channel_id=1, replica_groups=mesh['batch'=8,'cols'=4] {'batch'}, use_global_device_ids=true, to_apply=%region_30.0 | all-reduce | flops 2048 | bytes 16384 | tf_op jit(solution)/shard_map/psum | solution.py:65
  280.0 9.0 %all-gather = bf16[8,1,128]{2,1,0:T(2,128)(2,1)S(1)} all-gather(bf16[1,1,128]{2,1,0:T(2,128)(2,1)S(1)} %get-tuple-element.32), channel_id=1, replica_groups=mesh['batch'=8,'cols'=4] {'batch'}, dimensions={0}, use_global_device_ids=true | all-gather | bytes 2304 | tf_op jit(solution)/shard_map/all_gather | solution.py:135
  290.2 7.7 %all-gather.1 = bf16[8,1,128]{2,1,0:T(2,128)(2,1)S(1)} all-gather(bf16[1,1,128]{2,1,0:T(2,128)(2,1)S(1)} %get-tuple-element.30), channel_id=1, replica_groups=mesh['batch'=8,'cols'=4] {'batch'}, dimensions={0}, use_global_device_ids=true | all-gather | bytes 2304 | tf_op jit(solution)/shard_map/all_gather | solution.py:136
  299.2 10.9 %all_gather.26 = bf16[1024,256]{1,0:T(8,128)(2,1)S(1)} all-gather(bf16[128,256]{1,0:T(8,128)(2,1)S(1)} %get-tuple-element.40), channel_id=1, replica_groups=mesh['batch'=8,'cols'=4] {'batch'}, dimensions={0}, use_global_device_ids=true | all-gather | bytes 589824 | tf_op jit(solution)/shard_map/all_gather | solution.py:131
  310.9 11.7 %all_gather.27 = bf16[1024,256]{1,0:T(8,128)(2,1)S(1)} all-gather(bf16[128,256]{1,0:T(8,128)(2,1)S(1)} %get-tuple-element.38), channel_id=1, replica_groups=mesh['batch'=8,'cols'=4] {'batch'}, dimensions={0}, use_global_device_ids=true | all-gather | bytes 589824 | tf_op jit(solution)/shard_map/all_gather | solution.py:132
  323.3 9.5 %all_gather.28 = bf16[1024,256]{1,0:T(8,128)(2,1)S(1)} all-gather(bf16[128,256]{1,0:T(8,128)(2,1)S(1)} %get-tuple-element.36), channel_id=1, replica_groups=mesh['batch'=8,'cols'=4] {'batch'}, dimensions={0}, use_global_device_ids=true | all-gather | bytes 589824 | tf_op jit(solution)/shard_map/all_gather | solution.py:133
  333.5 9.3 %all_gather.29 = bf16[256,1024]{1,0:T(8,128)(2,1)S(1)} all-gather(bf16[256,128]{1,0:T(8,128)(2,1)S(1)} %get-tuple-element.34), channel_id=1, replica_groups=mesh['batch'=8,'cols'=4] {'batch'}, dimensions={1}, use_global_device_ids=true | all-gather | bytes 589824 | tf_op jit(solution)/shard_map/all_gather | solution.py:134
  342.8 3.2 copy.42
  346.0 1.3 copy.43
  (75 shorter events, 10.7 us)
Async XLA Ops:
  7.2 2.5 copy-start.3
  7.2 41.4 %reduce-scatter.21.cloned.1.call-start = ((), (), s32[]{:S(2)}) async-start(), calls=%async_computation.13 | async-start | bytes 589824
  8.6 2.0 copy-start.4
  9.7 1.9 copy-start.5
  9.7 76.8 %reduce-scatter.13.cloned.1.call-start = ((), (), s32[]{:S(2)}) async-start(), calls=%async_computation.9 | async-start | bytes 589824 | tf_op jit(solution)/shard_map/reduce_scatter | solution.py:40
  10.6 113.7 %reduce-scatter.15.cloned.1.call-start = ((), (), s32[]{:S(2)}) async-start(), calls=%async_computation.10 | async-start | bytes 589824 | tf_op jit(solution)/shard_map/reduce_scatter | solution.py:46
  11.5 150.4 %reduce-scatter.17.cloned.1.call-start = ((), (), s32[]{:S(2)}) async-start(), calls=%async_computation.11 | async-start | bytes 589824 | tf_op jit(solution)/shard_map/reduce_scatter | solution.py:52
  12.5 194.2 %reduce-scatter.19.cloned.1.call-start = ((), (), s32[]{:S(2)}) async-start(), calls=%async_computation.12 | async-start | bytes 2359296
  17.6 233.6 %reduce-scatter.11.cloned.1.call-start = ((), (), s32[]{:S(2)}) async-start(), calls=%async_computation.6 | async-start | bytes 2359296 | tf_op jit(solution)/shard_map/reduce_scatter | solution.py:28
  21.5 0.9 copy-start.6
  21.5 1.0 copy-start.7
  21.5 1.1 copy-start.8
  21.5 1.2 copy-start.9
  21.5 1.3 copy-start.1
  21.5 1.4 copy-start.2
  21.6 321.2 %all-gather.5.cloned.1.call-start = ((), (), s32[]{:S(2)}) async-start(), calls=%async_computation.7 | async-start | bytes 2359296 | tf_op jit(solution)/shard_map/all_gather | solution.py:129
  207.7 59.6 %copy-start.13 = (f32[1,1024]{1,0:T(1,128)S(1)}, f32[1,1024]{1,0:T(1,128)}, u32[]{:S(2)}) copy-start(f32[1,1024]{1,0:T(1,128)} %param.22) | copy-start | bytes 12292
  207.7 59.6 %copy-start.14 = (f32[1,1024]{1,0:T(1,128)S(1)}, f32[1,1024]{1,0:T(1,128)}, u32[]{:S(2)}) copy-start(f32[1,1024]{1,0:T(1,128)} %param.23) | copy-start | bytes 12292
  207.8 71.6 %copy-start.15 = (f32[128]{0:T(128)S(1)}, f32[128]{0:T(128)}, u32[]{:S(2)}) copy-start(f32[128]{0:T(128)} %param.30) | copy-start | bytes 1540
  207.8 81.8 %copy-start.16 = (f32[128]{0:T(128)S(1)}, f32[128]{0:T(128)}, u32[]{:S(2)}) copy-start(f32[128]{0:T(128)} %param.31) | copy-start | bytes 1540
  207.9 90.5 %copy-start.12 = (bf16[128,256]{1,0:T(8,128)(2,1)S(1)}, bf16[128,256]{1,0:T(8,128)(2,1)}, u32[]{:S(2)}) copy-start(bf16[128,256]{1,0:T(8,128)(2,1)} %reduce-scatter.13.cloned.1.call-done) | copy-start | bytes 196612
  264.2 45.9 %copy-start.10 = (bf16[128,256]{1,0:T(8,128)(2,1)S(1)}, bf16[128,256]{1,0:T(8,128)(2,1)}, u32[]{:S(2)}) copy-start(bf16[128,256]{1,0:T(8,128)(2,1)} %reduce-scatter.15.cloned.1.call-done) | copy-start | bytes 196612
  266.2 56.3 %copy-start.11 = (bf16[128,256]{1,0:T(8,128)(2,1)S(1)}, bf16[128,256]{1,0:T(8,128)(2,1)}, u32[]{:S(2)}) copy-start(bf16[128,256]{1,0:T(8,128)(2,1)} %reduce-scatter.17.cloned.1.call-done) | copy-start | bytes 196612
  266.2 76.5 %all-gather.7.cloned.1.call-start = ((), (), s32[]{:S(2)}) async-start(), calls=%async_computation.8 | async-start | bytes 2359296 | tf_op jit(solution)/shard_map/all_gather | solution.py:130
  342.8 3.2 copy-start
Sparse Core Ops, SparseCore 0:
  11.6 36.8 reduce-scatter.20
  52.2 34.1 reduce-scatter.12
  90.1 34.1 reduce-scatter.14
  127.8 34.1 reduce-scatter.16
  165.7 40.8 reduce-scatter.18
  210.3 40.8 reduce-scatter.10
  266.4 24.9 all-gather.4
  293.8 30.5 all-gather.6
where the time goes:
time: 358 us; the launch traced here: 357 us
  waiting for transfers between devices  223 us (62%)
  blocking collectives  81.9 us (23%)
  other arithmetic  23.3 us (7%)
  between operations  14.4 us (4%)
  local copies, waits for them, and re-layouts  14.3 us (4%)
    unnamed x10, waiting for transfers between devices  69.3 us
    reduce_scatter x1, waiting for transfers between devices, local(): lax.psum_scatter(grad_up[0].astype(jnp.float32).astype(jnp.bfloat16), 'ba...  43.3 us
    reduce_scatter x1, waiting for transfers between devices, local(): lax.psum_scatter(grad_key[0].astype(jnp.float32).astype(jnp.bfloat16), 'b...  36.9 us
    reduce_scatter x1, waiting for transfers between devices, local(): lax.psum_scatter(grad_query[0].astype(jnp.float32).astype(jnp.bfloat16),...  36.8 us
    reduce_scatter x1, waiting for transfers between devices, local(): lax.psum_scatter(grad_value[0].astype(jnp.float32).astype(jnp.bfloat16),...  36.7 us
    unnamed x44, local copies, waits for them, and re-layouts  14.3 us
    psum x1, blocking collectives, local(): lax.psum((grad_norm[0].astype(jnp.float32), grad_bias[0].astype(jnp.float...  12 us
    psum x1, blocking collectives, local(): lax.psum((jnp.sum(weight_up * weight_up, axis=1, keepdims=True), jnp.sum(...  11.8 us
  transfers between devices with their start and end apart: 8, of which 6 were waited for; matrix products, arithmetic and copies ran while one was open for 7% of the time, Pallas kernels for 0%

commit v1 on v0

--- a/solution.py
+++ b/solution.py
@@ -1,6 +1,10 @@
+import functools
+
 import jax
 import jax.numpy as jnp
 from jax import lax
+from jax.experimental import pallas as pl
+from jax.experimental.pallas import tpu as pltpu
 from jax.sharding import PartitionSpec as P
 
 learn_rate = 0.3
@@ -155,6 +159,469 @@
     )
 
 
+LANES = 128
+VMEM_BYTES = 48 * 1024 * 1024
+MESH = pl.DeviceIdType.MESH
+
+
+def gather_kernel(
+    n, nz, dims,
+    gu, gq, gk, gv, gd, gm, gnorm, gbias,
+    wu, wq, wk, wv, wd, wm, wnorm, wbias,
+    GR, GC, NR, NC, NV,
+    fu, fq, fk, fv, fd, fm,
+    vu, vq, vk, vv, vd, vm,
+    s0R, s0C, r0R, r0C, SR, SC, r1R, r1C, tR, tC, r2R, r2C,
+    vsend, vrecv, stm, st_send, st_recv,
+    load_sem, rs_send, rs_recv, z_send, z_recv, v_send, v_recv, ag_send, ag_recv,
+):
+    b = lax.axis_index("batch")
+    z = lax.axis_index("cols")
+    c, x, y = b % 2, (b // 2) % 2, b // 4
+    p_core, p_x, p_y = b + 1 - 2 * c, b + 2 - 4 * x, b + 4 - 8 * y
+    rows, up_w, at_w, dn_r, mx_r = dims
+    col_r = dn_r + mx_r
+    row_w = up_w + 3 * at_w
+    rate = n ** -0.5
+    segs = [(0, up_w)] + [(up_w + j * at_w, up_w + (j + 1) * at_w) for j in range(3)]
+    fR = (fu, fq, fk, fv)
+    hR = (gu, gq, gk, gv)
+    vR = (vu, vq, vk, vv)
+    other = 1 - c
+
+    loads = {}
+    count = [0]
+
+    def load(key, src, dst):
+        copy = pltpu.make_async_copy(src, dst, load_sem.at[count[0]])
+        count[0] += 1
+        copy.start()
+        loads.setdefault(key, []).append(copy)
+
+    for h in range(2):
+        for src, dst in zip(hR, fR):
+            load(("R", h, 0), src.at[:, other, h], dst.at[:, other, h])
+    for h in range(2):
+        load(("C", h), gd.at[h], fd.at[h])
+        load(("C", h), gm.at[h], fm.at[h])
+    for h in range(2):
+        for src, dst in zip(hR, fR):
+            load(("R", h, 1), src.at[:, c, h], dst.at[:, c, h])
+    for src, dst in ((wu, vu), (wq, vq), (wk, vk), (wv, vv)):
+        load("wR", src, dst)
+    for src, dst in ((wd, vd), (wm, vm)):
+        load("wC", src, dst)
+
+    def ready(key):
+        for copy in loads[key]:
+            copy.wait()
+
+    barrier = pltpu.get_barrier_semaphore()
+    for d in range(1, n):
+        pl.semaphore_signal(barrier, inc=1, device_id={"batch": (b + d) % n}, device_id_type=MESH)
+    for d in range(1, nz):
+        pl.semaphore_signal(barrier, inc=1, device_id={"cols": (z + d) % nz}, device_id_type=MESH)
+    pl.semaphore_wait(barrier, n - 1 + nz - 1)
+
+    def remote(src, dst, send, recv, axis, target):
+        return pltpu.make_async_remote_copy(
+            src_ref=src, dst_ref=dst, send_sem=send, recv_sem=recv,
+            device_id={axis: target}, device_id_type=MESH,
+        )
+
+    pending = []
+
+    for o in range(n):
+        vsend[o, 0:1, :] = gnorm[0:1, o * LANES : (o + 1) * LANES]
+        vsend[o, 1:2, :] = gbias[0:1, o * LANES : (o + 1) * LANES]
+    vec_in = []
+    for d in range(1, n):
+        to = (b + d) % n
+        copy = remote(vsend.at[to], vrecv.at[d], v_send.at[0, d], v_recv.at[0, d], "batch", to)
+        copy.start()
+        vec_in.append(copy)
+
+    STEP = 16
+    per = rows // STEP
+    CSTEP = 128
+    n_dn, n_mx = dn_r // CSTEP, mx_r // CSTEP
+
+    def piece(h, q, core, part):
+        return pl.ds(pl.multiple_of((2 * q + core) * LANES, LANES), LANES)
+
+    chunks = [("R", 0), ("R", 1), ("C", 0), ("C", 1)]
+    core_copies = []
+    for i, (kind, h) in enumerate(chunks):
+        if kind == "R":
+            ready(("R", h, 0))
+
+            def cast(t, _, h=h):
+                q, r = t // per, pl.ds(pl.multiple_of((t % per) * STEP, STEP), STEP)
+                for (lo, hi), f in zip(segs, fR):
+                    s0R[h, q, r, lo:hi] = f[q, other, h, r, :].astype(jnp.bfloat16)
+                return 0
+
+            lax.fori_loop(0, n // 2 * per, cast, 0)
+            copy = remote(s0R.at[h], r0R.at[h], rs_send.at[0, i], rs_recv.at[0, i], "batch", p_core)
+        else:
+            ready(("C", h))
+
+            def cast(q, _, h=h):
+                lanes = piece(h, q, other, 0)
+                for k in range(n_dn):
+                    r = slice(k * CSTEP, (k + 1) * CSTEP)
+                    s0C[h, q, r, :] = fd[h, r, lanes].astype(jnp.bfloat16)
+                for k in range(n_mx):
+                    r = slice(k * CSTEP, (k + 1) * CSTEP)
+                    s0C[h, q, dn_r + k * CSTEP : dn_r + (k + 1) * CSTEP, :] = fm[h, r, lanes].astype(jnp.bfloat16)
+                return 0
+
+            lax.fori_loop(0, n // 2, cast, 0)
+            copy = remote(s0C.at[h], r0C.at[h], rs_send.at[0, i], rs_recv.at[0, i], "batch", p_core)
+        copy.start()
+        core_copies.append(copy)
+        pending.append(copy)
+
+    first = []
+    for i, (kind, h) in enumerate(chunks):
+        core_copies[i].wait_recv()
+        if kind == "R":
+            ready(("R", h, 1))
+
+            def add(t, _, h=h):
+                q, r = t // per, pl.ds(pl.multiple_of((t % per) * STEP, STEP), STEP)
+                for (lo, hi), f in zip(segs, fR):
+                    both = f[q, c, h, r, :] + r0R[h, q, r, lo:hi].astype(jnp.float32)
+                    SR[h, q // 2, q % 2, r, lo:hi] = both.astype(jnp.bfloat16)
+                return 0
+
+            lax.fori_loop(0, n // 2 * per, add, 0)
+            S, r1 = SR, r1R
+        else:
+
+            def add(q, _, h=h):
+                lanes = piece(h, q, c, 0)
+                for f, base, blocks in ((fd, 0, n_dn), (fm, dn_r, n_mx)):
+                    for k in range(blocks):
+                        here = slice(base + k * CSTEP, base + (k + 1) * CSTEP)
+                        both = f[h, k * CSTEP : (k + 1) * CSTEP, lanes] + r0C[h, q, here, :].astype(jnp.float32)
+                        SC[h, q // 2, q % 2, here, :] = both.astype(jnp.bfloat16)
+                return 0
+
+            lax.fori_loop(0, n // 2, add, 0)
+            S, r1 = SC, r1C
+        if h == 0:
+            src, target = S.at[h, :, 1 - x], p_x
+        else:
+            src, target = S.at[h, 1 - y], p_y
+        copy = remote(src, r1.at[h], rs_send.at[1, i], rs_recv.at[1, i], "batch", target)
+        copy.start()
+        first.append(copy)
+        pending.append(copy)
+
+    second = []
+    for i, (kind, h) in enumerate(chunks):
+        first[i].wait_recv()
+        yy, xx, away, target = (1 - y, x, 1 - y, p_y) if h == 0 else (y, 1 - x, 1 - x, p_x)
+        S, r1, t_, r2, blk, steps = (
+            (SR, r1R, tR, r2R, STEP, per) if kind == "R" else (SC, r1C, tC, r2C, CSTEP, n_dn + n_mx)
+        )
+
+        def fold(k, _, h=h, yy=yy, xx=xx, away=away, S=S, r1=r1, t_=t_, blk=blk):
+            r = pl.ds(pl.multiple_of(k * blk, blk), blk)
+            both = S[h, yy, xx, r, :].astype(jnp.float32) + r1[h, away, r, :].astype(jnp.float32)
+            t_[h, r, :] = both.astype(jnp.bfloat16)
+            return 0
+
+        lax.fori_loop(0, steps, fold, 0)
+        copy = remote(t_.at[h], r2.at[h], rs_send.at[2, i], rs_recv.at[2, i], "batch", target)
+        copy.start()
+        second.append(copy)
+        pending.append(copy)
+
+    def mean_of(S, r1, r2, h, r):
+        near = y if h == 0 else x
+        total = S[h, y, x, r, :].astype(jnp.float32) + r1[h, near, r, :].astype(jnp.float32)
+        return (total + r2[h, r, :].astype(jnp.float32)) * rate
+
+    def spread(slot):
+        copies = []
+        for d in range(1, nz):
+            copy = remote(
+                st_send.at[slot], st_recv.at[slot, d], z_send.at[slot, d], z_recv.at[slot, d], "cols", (z + d) % nz
+            )
+            copy.start()
+            copies.append(copy)
+        return copies
+
+    ready("wR")
+    lane = lax.broadcasted_iota(jnp.int32, (STEP, LANES), 1)
+    for h in range(2):
+        second[h].wait_recv()
+
+        def means(k, _, h=h):
+            r = pl.ds(pl.multiple_of(k * STEP, STEP), STEP)
+            mean = mean_of(SR, r1R, r2R, h, r)
+            NR[h, r, :] = mean
+            stats = jnp.zeros((STEP, LANES), jnp.float32)
+            for j, ((lo, hi), v) in enumerate(zip(segs, vR)):
+                w = v[h, r, :]
+                own = jnp.sum(w * w, axis=1, keepdims=True)
+                m = mean[:, lo:hi]
+                slope = jnp.sum(m * m, axis=1, keepdims=True)
+                stats = jnp.where(lane == j, own, stats)
+                stats = jnp.where(lane == 4 + j, slope, stats)
+            stm[pl.ds(pl.multiple_of(h * rows + k * STEP, STEP), STEP), :] = stats
+            return 0
+
+        lax.fori_loop(0, per, means, 0)
+    st_send[0] = jnp.transpose(stm[...])[0:8, :]
+    z_row = spread(0)
+
+    total = vsend[b]
+    for copy in vec_in:
+        copy.wait_recv()
+    for d in range(1, n):
+        total = total + vrecv[d]
+    old = jnp.concatenate([wnorm[...], wbias[...]], axis=0)
+    NV[b] = old - learn_rate * (total * rate)
+    vec_out = []
+    for d in range(1, n):
+        copy = remote(NV.at[b], NV.at[b], v_send.at[1, d], v_recv.at[1, d], "batch", (b + d) % n)
+        copy.start()
+        vec_out.append(copy)
+
+    ready("wC")
+    zero = jnp.zeros((1, LANES), jnp.float32)
+    sums = [zero] * 4
+    for h in range(2):
+        second[2 + h].wait_recv()
+
+        def means(k, carry, h=h, v=None, base=0):
+            r = pl.ds(pl.multiple_of(base + k * CSTEP, CSTEP), CSTEP)
+            mean = mean_of(SC, r1C, r2C, h, r)
+            NC[h, r, :] = mean
+            w = v[h, pl.ds(pl.multiple_of(k * CSTEP, CSTEP), CSTEP), :]
+            own, slope = carry
+            return (
+                own + jnp.sum(w * w, axis=0, keepdims=True),
+                slope + jnp.sum(mean * mean, axis=0, keepdims=True),
+            )
+
+        sums[0], sums[2] = lax.fori_loop(
+            0, n_dn, functools.partial(means, v=vd, base=0), (sums[0], sums[2])
+        )
+        sums[1], sums[3] = lax.fori_loop(
+            0, n_mx, functools.partial(means, v=vm, base=dn_r), (sums[1], sums[3])
+        )
+    st_send[1] = jnp.concatenate(sums + [zero] * 4, axis=0)
+    z_col = spread(1)
+
+    def ratio_of(slot, copies, number):
+        for copy in copies:
+            copy.wait_recv()
+        total = st_send[slot]
+        for d in range(1, nz):
+            total = total + st_recv[slot, d]
+        return jnp.sqrt(total[0:number]) * lax.rsqrt(total[number : 2 * number] + 1e-06)
+
+    ag = {}
+
+    def share(i, G, slot, step, axis_target):
+        copy = remote(
+            G.at[slot, chunks[i][1]], G.at[slot, chunks[i][1]],
+            ag_send.at[i, step], ag_recv.at[i, step], "batch", axis_target,
+        )
+        copy.start()
+        ag[i, step] = copy
+
+    def own_out(i, G):
+        h = chunks[i][1]
+        near, far = (p_y, p_x) if h == 0 else (p_x, p_y)
+        share(i, G, b, 0, near)
+        share(i, G, b, 1, far)
+        share(i, G, b, 3, p_core)
+
+    ratio = ratio_of(0, z_row, 4)
+    stm[...] = jnp.transpose(jnp.concatenate([ratio, jnp.zeros((LANES - 4, LANES), jnp.float32)], axis=0))
+    for h in range(2):
+
+        def update(k, _, h=h):
+            r = pl.ds(pl.multiple_of(k * STEP, STEP), STEP)
+            scale = stm[pl.ds(pl.multiple_of(h * rows + k * STEP, STEP), STEP), :]
+            for j, ((lo, hi), v) in enumerate(zip(segs, vR)):
+                new = v[h, r, :] - learn_rate * (NR[h, r, lo:hi] * scale[:, j : j + 1])
+                NR[h, r, lo:hi] = new
+                GR[b, h, r, lo:hi] = new.astype(jnp.bfloat16)
+            return 0
+
+        lax.fori_loop(0, per, update, 0)
+        own_out(h, GR)
+
+    ratio = ratio_of(1, z_col, 2)
+    for h in range(2):
+        for j, (v, base, blocks) in enumerate(((vd, 0, n_dn), (vm, dn_r, n_mx))):
+
+            def update(k, _, h=h, j=j, v=v, base=base):
+                r = pl.ds(pl.multiple_of(base + k * CSTEP, CSTEP), CSTEP)
+                w = v[h, pl.ds(pl.multiple_of(k * CSTEP, CSTEP), CSTEP), :]
+                new = w - learn_rate * (NC[h, r, :] * ratio[j : j + 1, :])
+                NC[h, r, :] = new
+                GC[b, h, r, :] = new.astype(jnp.bfloat16)
+                return 0
+
+            lax.fori_loop(0, blocks, update, 0)
+        own_out(2 + h, GC)
+
+    for pair in ((0, 1), (2, 3)):
+        for i in pair:
+            h, G = chunks[i][1], GR if i < 2 else GC
+            near, far = (p_y, p_x) if h == 0 else (p_x, p_y)
+            ag[i, 0].wait_recv()
+            share(i, G, near, 2, far)
+            share(i, G, near, 4, p_core)
+        for i in pair:
+            h, G = chunks[i][1], GR if i < 2 else GC
+            far = p_x if h == 0 else p_y
+            ag[i, 1].wait_recv()
+            share(i, G, far, 5, p_core)
+    across = p_x + p_y - b
+    for i in range(4):
+        ag[i, 2].wait_recv()
+        share(i, GR if i < 2 else GC, across, 6, p_core)
+    for i in range(4):
+        for step in range(3, 7):
+            ag[i, step].wait_recv()
+        for step in range(7):
+            ag[i, step].wait_send()
+    for copy in vec_out:
+        copy.wait_recv()
+        copy.wait_send()
+    for copy in vec_in + z_row + z_col + pending:
+        copy.wait_send()
+
+
+def write_kernel(dims, GR, GC, NR, NC, NV, cu, cd, cq, ck, cv, cm, cn, cb, nu, nd, nq, nk, nv, nm, nn, nb, sem):
+    rows, up_w, at_w, dn_r, mx_r = dims
+    n = GR.shape[0]
+    b = lax.axis_index("batch")
+    copies = []
+
+    def go(src, dst):
+        copy = pltpu.make_async_copy(src, dst, sem.at[len(copies)])
+        copy.start()
+        copies.append(copy)
+
+    for o in range(n):
+        lanes = pl.ds(o * LANES, LANES)
+        go(GC.at[o, :, 0:dn_r, :], cd.at[:, :, lanes])
+        go(GC.at[o, :, dn_r : dn_r + mx_r, :], cm.at[:, :, lanes])
+    go(GR.at[:, :, :, 0:up_w], cu)
+    go(NR.at[:, :, 0:up_w], nu)
+    for j, (copied, new) in enumerate(((cq, nq), (ck, nk), (cv, nv))):
+        lanes = slice(up_w + j * at_w, up_w + (j + 1) * at_w)
+        go(GR.at[:, :, :, lanes], copied)
+        go(NR.at[:, :, lanes], new)
+    go(NC.at[:, 0:dn_r], nd)
+    go(NC.at[:, dn_r : dn_r + mx_r], nm)
+    for o in range(n):
+        both = NV[o]
+        cn[0:1, o * LANES : (o + 1) * LANES] = both[0:1].astype(jnp.bfloat16)
+        cb[0:1, o * LANES : (o + 1) * LANES] = both[1:2].astype(jnp.bfloat16)
+    own = NV[b]
+    nn[...] = own[0:1]
+    nb[...] = own[1:2]
+    for copy in copies:
+        copy.wait()
+
+
+def fused(
+    grad_up, grad_down, grad_query, grad_key, grad_value, grad_mixed, grad_norm, grad_bias,
+    weight_up, weight_down, weight_query, weight_key, weight_value, weight_mixed, weight_norm, weight_bias,
+):
+    n, nz = lax.axis_size("batch"), lax.axis_size("cols")
+    f32, bf16 = jnp.float32, jnp.bfloat16
+    rows = weight_up.shape[0] // 2
+    up_w, at_w = weight_up.shape[1], weight_query.shape[1]
+    dn_r, mx_r = weight_down.shape[0] // 2, weight_mixed.shape[0] // 2
+    dims = (rows, up_w, at_w, dn_r, mx_r)
+    row_w, col_r = up_w + 3 * at_w, dn_r + mx_r
+    chips = n // 2
+
+    def by_row(g):
+        return g[0].reshape(chips, 2, 2, rows, g.shape[2])
+
+    def halves(a):
+        return a.reshape(2, a.shape[0] // 2, a.shape[1])
+
+    ANY = pl.BlockSpec(memory_space=pl.ANY)
+    VM = pl.BlockSpec(memory_space=pltpu.VMEM)
+    DMA = pltpu.SemaphoreType.DMA
+    mid = [
+        jax.ShapeDtypeStruct((n, 2, rows, row_w), bf16),
+        jax.ShapeDtypeStruct((n, 2, col_r, LANES), bf16),
+        jax.ShapeDtypeStruct((2, rows, row_w), f32),
+        jax.ShapeDtypeStruct((2, col_r, LANES), f32),
+        jax.ShapeDtypeStruct((n, 2, LANES), f32),
+    ]
+    scratch = [pltpu.VMEM((chips, 2, 2, rows, w), f32) for w in (up_w, at_w, at_w, at_w)]
+    scratch += [pltpu.VMEM((2, r, n * LANES), f32) for r in (dn_r, mx_r)]
+    scratch += [pltpu.VMEM((2, rows, w), f32) for w in (up_w, at_w, at_w, at_w)]
+    scratch += [pltpu.VMEM((2, r, LANES), f32) for r in (dn_r, mx_r)]
+    R, C = (rows, row_w), (col_r, LANES)
+    for lead in ((2, chips), (2, chips), (2, 2, 2), (2, 2), (2,), (2,)):
+        scratch += [pltpu.VMEM(lead + R, bf16), pltpu.VMEM(lead + C, bf16)]
+    scratch += [
+        pltpu.VMEM((n, 2, LANES), f32),
+        pltpu.VMEM((n, 2, LANES), f32),
+        pltpu.VMEM((2 * rows, LANES), f32),
+        pltpu.VMEM((2, 8, LANES), f32),
+        pltpu.VMEM((2, nz, 8, LANES), f32),
+        DMA((26,)), DMA((3, 4)), DMA((3, 4)), DMA((2, nz)), DMA((2, nz)),
+        DMA((2, n)), DMA((2, n)), DMA((4, 7)), DMA((4, 7)),
+    ]
+    got = pl.pallas_call(
+        functools.partial(gather_kernel, n, nz, dims),
+        out_shape=mid,
+        in_specs=[ANY] * 6 + [VM] * 2 + [ANY] * 6 + [VM] * 2,
+        out_specs=[VM] * 5,
+        scratch_shapes=scratch,
+        compiler_params=pltpu.CompilerParams(
+            collective_id=0, has_side_effects=True, vmem_limit_bytes=VMEM_BYTES
+        ),
+        name="sum_and_share",
+    )(
+        by_row(grad_up), by_row(grad_query), by_row(grad_key), by_row(grad_value),
+        halves(grad_down[0]), halves(grad_mixed[0]), grad_norm, grad_bias,
+        halves(weight_up), halves(weight_query), halves(weight_key), halves(weight_value),
+        halves(weight_down), halves(weight_mixed), weight_norm[None], weight_bias[None],
+    )
+    S = jax.ShapeDtypeStruct
+    width = n * LANES
+    outs = pl.pallas_call(
+        functools.partial(write_kernel, dims),
+        out_shape=[
+            S((n, 2, rows, up_w), bf16), S((2, dn_r, width), bf16),
+            S((n, 2, rows, at_w), bf16), S((n, 2, rows, at_w), bf16), S((n, 2, rows, at_w), bf16),
+            S((2, mx_r, width), bf16), S((1, width), bf16), S((1, width), bf16),
+            S((2, rows, up_w), f32), S((2, dn_r, LANES), f32),
+            S((2, rows, at_w), f32), S((2, rows, at_w), f32), S((2, rows, at_w), f32),
+            S((2, mx_r, LANES), f32), S((1, LANES), f32), S((1, LANES), f32),
+        ],
+        in_specs=[VM] * 5,
+        out_specs=[ANY] * 6 + [VM] * 2 + [ANY] * 6 + [VM] * 2,
+        scratch_shapes=[DMA((26,))],
+        name="write_out",
+    )(*got)
+    shapes = [
+        (n * 2 * rows, up_w), (2 * dn_r, width), (n * 2 * rows, at_w), (n * 2 * rows, at_w),
+        (n * 2 * rows, at_w), (2 * mx_r, width), (width,), (width,),
+        weight_up.shape, weight_down.shape, weight_query.shape, weight_key.shape,
+        weight_value.shape, weight_mixed.shape, weight_norm.shape, weight_bias.shape,
+    ]
+    return tuple(out.reshape(shape) for out, shape in zip(outs, shapes))
+
+
 def solution(mesh):
     in_specs = (
         P("batch", None, "cols"),
@@ -192,4 +659,13 @@
         P("batch"),
         P("batch"),
     )
-    return jax.shard_map(local, mesh=mesh, in_specs=in_specs, out_specs=out_specs, check_vma=False)
+    whole = mesh.shape["batch"]
+
+    def chosen(*arrays):
+        width = arrays[15].shape[0]
+        fits = whole == 8 and width == LANES and all(
+            side % LANES == 0 for array in arrays[:6] for side in array.shape[1:]
+        )
+        return (fused if fits else local)(*arrays)
+
+    return jax.shard_map(chosen, mesh=mesh, in_specs=in_specs, out_specs=out_specs, check_vma=False)

time: 358 us -> 96 us (0.27)
  waiting for transfers between devices: 223 us -> 0 us
  blocking collectives: 81.9 us -> 0 us
  Pallas kernels: 0 us -> 79.1 us
  other arithmetic: 23.3 us -> 2.56 us
  between operations: 14.4 us -> 0.7 us
    reduce_scatter x4 -> x0, waiting for transfers between devices: 154 us -> none  [the longest x1 43.3 us: local(): lax.psum_scatter(grad_up[0].astype(jnp.float32).astype(jnp.bfloat16), 'ba...]
    pallas_call x0 -> x2, Pallas kernels: none -> 79.1 us  [the longest x1 71.9 us: fused(): pl.pallas_call(functools.partial(gather_kernel, n, nz, dims), out_shape=m...]
    unnamed x10 -> x0, waiting for transfers between devices: 69.3 us -> none
    all_gather x6 -> x0, blocking collectives: 58.1 us -> none  [the longest x1 11.7 us: local(): lax.all_gather(new_key.astype(jnp.bfloat16), 'batch', axis=0, tiled=True)]
    psum x2 -> x0, blocking collectives: 23.9 us -> none  [the longest x1 12 us: local(): lax.psum((grad_norm[0].astype(jnp.float32), grad_bias[0].astype(jnp.float...]
    convert_element_type x12 -> x0, other arithmetic: 16.1 us -> none  [the longest x1 3.84 us: local(): grad_up[0].astype(jnp.float32).astype(jnp.bfloat16)]
    reduce_sum x12 -> x0, other arithmetic: 4.76 us -> none  [the longest x1 1.1 us: local(): jnp.sum(mean_up * mean_up, axis=1, keepdims=True)]
    unnamed x44 -> x30, local copies, waits for them, and re-layouts: 14.3 us -> 13.2 us
  transfers between devices with their start and end apart: 8 -> 0, of which waited for: 6 -> 0; matrix products, arithmetic and copies ran while one was open for 7% -> 0% of each run, Pallas kernels for 0% -> 0%
where the time goes in v1:
time: 96 us; the launch traced here: 95.5 us
  Pallas kernels  79.1 us (82%)
  local copies, waits for them, and re-layouts  13.2 us (14%)
  other arithmetic  2.56 us (3%)
    pallas_call x1, Pallas kernels, fused(): pl.pallas_call(functools.partial(gather_kernel, n, nz, dims), out_shape=m...  71.9 us
    unnamed x30, local copies, waits for them, and re-layouts  13.2 us
    pallas_call x1, Pallas kernels, fused(): pl.pallas_call(functools.partial(write_kernel, dims), out_shape=[S((n, 2,...  7.16 us
    pallas_call x2, other arithmetic, fused(): pl.pallas_call(functools.partial(write_kernel, dims), out_shape=[S((n, 2,...  2.56 us

profile of v1, /device:TPU:0, one launch (start us, length us, event | category | flops | bytes accessed | tf_op | source)
XLA Modules:
  0.0 95.5 jit_solution(17620366062321551592)
XLA Ops:
  0.7 0.0 copy-start
  0.7 1.2 %copy-done = f32[1,1024,256]{2,1,0:T(8,128)S(1)} copy-done((f32[1,1024,256]{2,1,0:T(8,128)S(1)}, f32[1,1024,256]{2,1,0:T(8,128)}, u32[]{:S(2)}) %copy-start) | copy-done | bytes 1048600
  1.9 0.0 copy-start.1
  1.9 1.2 %copy-done.1 = f32[1,1024,256]{2,1,0:T(8,128)S(1)} copy-done((f32[1,1024,256]{2,1,0:T(8,128)S(1)}, f32[1,1024,256]{2,1,0:T(8,128)}, u32[]{:S(2)}) %copy-start.1) | copy-done | bytes 1048600
  3.1 0.0 copy-start.4
  3.1 1.0 %copy-done.4 = f32[128,1024]{1,0:T(8,128)S(1)} copy-done((f32[128,1024]{1,0:T(8,128)S(1)}, f32[128,1024]{1,0:T(8,128)}, u32[]{:S(2)}) %copy-start.4) | copy-done | bytes 524312
  4.1 0.0 copy-start.5
  4.1 1.0 %copy-done.5 = f32[1024,128]{1,0:T(8,128)S(1)} copy-done((f32[1024,128]{1,0:T(8,128)S(1)}, f32[1024,128]{1,0:T(8,128)}, u32[]{:S(2)}) %copy-start.5) | copy-done | bytes 524312
  5.2 0.0 copy-start.6
  5.2 0.9 copy-done.6
  6.1 0.0 copy-start.7
  6.1 0.9 copy-done.7
  7.0 0.0 copy-start.8
  7.0 0.9 copy-done.8
  7.9 0.0 copy-start.9
  7.9 0.9 copy-done.9
  8.8 0.0 copy-start.11
  8.8 0.7 copy-done.11
  9.5 0.0 copy-start.12
  9.5 0.7 copy-done.12
  10.2 0.0 copy-start.13
  10.2 0.7 copy-done.13
  10.8 0.0 copy-start.14
  10.8 0.7 copy-done.14
  11.5 71.9 %sum_and_share.1 = (bf16[8,2,64,1792]{3,2,1,0:T(8,128)(2,1)}, bf16[8,2,640,128]{3,2,1,0:T(8,128)(2,1)}, f32[2,64,1792]{2,1,0:T(8,128)S(1)}, f32[2,640,128]{2,1,0:T(8,128)S(1)}, f32[8,2,128]{2,1,0:T(2,128)S(1)}) custom-call(f32[4,2,2,64,1024]{4,3,2,1,0:T(8,128)} %bitcast.38, f32[4,2,2,64,256]{4,3,2,1,0:T(8,128)S(1)} %bitcast.28, ...), custom_call_target="tpu_custom_call" | custom-call | tf_op jit(solution)/shard_map/sum_and_share/pallas_call | solution.py:583
  83.4 0.0 copy-start.2
  83.4 1.0 copy-done.2
  84.4 0.8 copy-done.3
  85.2 0.6 copy-done.10
  85.8 7.2 %write_out.1 = (bf16[8,2,64,1024]{3,2,1,0:T(8,128)(2,1)}, bf16[2,512,1024]{2,1,0:T(8,128)(2,1)}, bf16[8,2,64,256]{3,2,1,0:T(8,128)(2,1)}, bf16[8,2,64,256]{3,2,1...) custom-call(bf16[8,2,64,1792]{3,2,1,0:T(8,128)(2,1)} %get-tuple-elem, ...), custom_call_target="tpu_custom_call" | custom-call | tf_op jit(solution)/shard_map/write_out/pallas_call | solution.py:601
  93.0 1.3 %reduce = bf16[1024]{0:T(1024)(128)(2,1)} reduce(bf16[1,1024]{1,0:T(2,128)(2,1)} %get-tuple-element.48, bf16[]{:T(256)} %constant.8), dimensions={0}, to_apply=%get-tuple-element.48.reduce_sub_computation | reduce | bytes 4098 | tf_op jit(solution)/shard_map/write_out/pallas_call | solution.py:601
  94.3 1.3 %reduce.1 = bf16[1024]{0:T(1024)(128)(2,1)} reduce(bf16[1,1024]{1,0:T(2,128)(2,1)} %get-tuple-element.49, bf16[]{:T(256)} %constant.8), dimensions={0}, to_apply=%get-tuple-element.49.reduce_sub_computation | reduce | bytes 4098 | tf_op jit(solution)/shard_map/write_out/pallas_call | solution.py:601
  (2 shorter events, 0.0 us)
Async XLA Ops:
  0.7 1.2 %copy-start = (f32[1,1024,256]{2,1,0:T(8,128)S(1)}, f32[1,1024,256]{2,1,0:T(8,128)}, u32[]{:S(2)}) copy-start(f32[1,1024,256]{2,1,0:T(8,128)} %param.18) | copy-start | bytes 3145732
  1.9 1.2 %copy-start.1 = (f32[1,1024,256]{2,1,0:T(8,128)S(1)}, f32[1,1024,256]{2,1,0:T(8,128)}, u32[]{:S(2)}) copy-start(f32[1,1024,256]{2,1,0:T(8,128)} %param.19) | copy-start | bytes 3145732
  3.1 1.0 %copy-start.4 = (f32[128,1024]{1,0:T(8,128)S(1)}, f32[128,1024]{1,0:T(8,128)}, u32[]{:S(2)}) copy-start(f32[128,1024]{1,0:T(8,128)} %param.24) | copy-start | bytes 1572868
  4.1 1.0 %copy-start.5 = (f32[1024,128]{1,0:T(8,128)S(1)}, f32[1024,128]{1,0:T(8,128)}, u32[]{:S(2)}) copy-start(f32[1024,128]{1,0:T(8,128)} %param.25) | copy-start | bytes 1572868
  5.2 0.9 copy-start.6
  6.1 0.9 copy-start.7
  7.0 0.9 copy-start.8
  7.9 0.9 copy-start.9
  8.8 0.7 copy-start.11
  9.5 0.7 copy-start.12
  10.2 0.7 copy-start.13
  10.8 0.7 copy-start.14
  83.4 1.0 %copy-start.2 = (f32[2,64,1792]{2,1,0:T(8,128)}, f32[2,64,1792]{2,1,0:T(8,128)S(1)}, u32[]{:S(2)}) copy-start(f32[2,64,1792]{2,1,0:T(8,128)S(1)} %get-tuple-element.39.NR) | copy-start | bytes 2752516
  84.4 0.8 copy-start.3
  85.2 0.6 copy-start.10

commit v2 on v1

--- a/solution.py
+++ b/solution.py
@@ -160,20 +160,20 @@
 
 
 LANES = 128
-VMEM_BYTES = 48 * 1024 * 1024
+VMEM_BYTES = 40 * 1024 * 1024
 MESH = pl.DeviceIdType.MESH
 
 
 def gather_kernel(
     n, nz, dims,
-    gu, gq, gk, gv, gd, gm, gnorm, gbias,
-    wu, wq, wk, wv, wd, wm, wnorm, wbias,
+    gu, gq, gk, gv, gd, gm, hnorm, hbias,
+    wu, wq, wk, wv, wd, wm, knorm, kbias,
     GR, GC, NR, NC, NV,
     fu, fq, fk, fv, fd, fm,
     vu, vq, vk, vv, vd, vm,
     s0R, s0C, r0R, r0C, SR, SC, r1R, r1C, tR, tC, r2R, r2C,
     vsend, vrecv, stm, st_send, st_recv,
-    load_sem, rs_send, rs_recv, z_send, z_recv, v_send, v_recv, ag_send, ag_recv,
+    gnorm, gbias, wnorm, wbias, load_sem, rs_send, rs_recv, z_send, z_recv, v_send, v_recv, ag_send, ag_recv,
 ):
     b = lax.axis_index("batch")
     z = lax.axis_index("cols")
@@ -198,6 +198,8 @@
         copy.start()
         loads.setdefault(key, []).append(copy)
 
+    for src, dst in ((hnorm, gnorm), (hbias, gbias), (knorm, wnorm), (kbias, wbias)):
+        load("v", src, dst)
     for h in range(2):
         for src, dst in zip(hR, fR):
             load(("R", h, 0), src.at[:, other, h], dst.at[:, other, h])
@@ -231,6 +233,7 @@
 
     pending = []
 
+    ready("v")
     for o in range(n):
         vsend[o, 0:1, :] = gnorm[0:1, o * LANES : (o + 1) * LANES]
         vsend[o, 1:2, :] = gbias[0:1, o * LANES : (o + 1) * LANES]
@@ -554,15 +557,15 @@
     def halves(a):
         return a.reshape(2, a.shape[0] // 2, a.shape[1])
 
-    ANY = pl.BlockSpec(memory_space=pl.ANY)
+    HB = pl.BlockSpec(memory_space=pltpu.MemorySpace.HBM)
     VM = pl.BlockSpec(memory_space=pltpu.VMEM)
     DMA = pltpu.SemaphoreType.DMA
     mid = [
-        jax.ShapeDtypeStruct((n, 2, rows, row_w), bf16),
-        jax.ShapeDtypeStruct((n, 2, col_r, LANES), bf16),
-        jax.ShapeDtypeStruct((2, rows, row_w), f32),
-        jax.ShapeDtypeStruct((2, col_r, LANES), f32),
-        jax.ShapeDtypeStruct((n, 2, LANES), f32),
+        pltpu.VMEM((n, 2, rows, row_w), bf16),
+        pltpu.VMEM((n, 2, col_r, LANES), bf16),
+        pltpu.VMEM((2, rows, row_w), f32),
+        pltpu.VMEM((2, col_r, LANES), f32),
+        pltpu.VMEM((n, 2, LANES), f32),
     ]
     scratch = [pltpu.VMEM((chips, 2, 2, rows, w), f32) for w in (up_w, at_w, at_w, at_w)]
     scratch += [pltpu.VMEM((2, r, n * LANES), f32) for r in (dn_r, mx_r)]
@@ -577,25 +580,27 @@
         pltpu.VMEM((2 * rows, LANES), f32),
         pltpu.VMEM((2, 8, LANES), f32),
         pltpu.VMEM((2, nz, 8, LANES), f32),
-        DMA((26,)), DMA((3, 4)), DMA((3, 4)), DMA((2, nz)), DMA((2, nz)),
+        pltpu.VMEM((1, n * LANES), f32), pltpu.VMEM((1, n * LANES), f32),
+        pltpu.VMEM((1, LANES), f32), pltpu.VMEM((1, LANES), f32),
+        DMA((30,)), DMA((3, 4)), DMA((3, 4)), DMA((2, nz)), DMA((2, nz)),
         DMA((2, n)), DMA((2, n)), DMA((4, 7)), DMA((4, 7)),
     ]
     got = pl.pallas_call(
         functools.partial(gather_kernel, n, nz, dims),
         out_shape=mid,
-        in_specs=[ANY] * 6 + [VM] * 2 + [ANY] * 6 + [VM] * 2,
+        in_specs=[HB] * 16,
         out_specs=[VM] * 5,
         scratch_shapes=scratch,
         compiler_params=pltpu.CompilerParams(
             collective_id=0, has_side_effects=True, vmem_limit_bytes=VMEM_BYTES
         ),
         name="sum_and_share",
-    )(
+    )(*(pltpu.with_memory_space_constraint(a, pltpu.MemorySpace.HBM) for a in (
         by_row(grad_up), by_row(grad_query), by_row(grad_key), by_row(grad_value),
         halves(grad_down[0]), halves(grad_mixed[0]), grad_norm, grad_bias,
         halves(weight_up), halves(weight_query), halves(weight_key), halves(weight_value),
         halves(weight_down), halves(weight_mixed), weight_norm[None], weight_bias[None],
-    )
+    )))
     S = jax.ShapeDtypeStruct
     width = n * LANES
     outs = pl.pallas_call(
@@ -609,10 +614,11 @@
             S((2, mx_r, LANES), f32), S((1, LANES), f32), S((1, LANES), f32),
         ],
         in_specs=[VM] * 5,
-        out_specs=[ANY] * 6 + [VM] * 2 + [ANY] * 6 + [VM] * 2,
+        out_specs=[HB] * 6 + [VM] * 2 + [HB] * 6 + [VM] * 2,
         scratch_shapes=[DMA((26,))],
+        compiler_params=pltpu.CompilerParams(vmem_limit_bytes=VMEM_BYTES // 10),
         name="write_out",
-    )(*got)
+    )(*(pltpu.with_memory_space_constraint(a, pltpu.MemorySpace.VMEM) for a in got))
     shapes = [
         (n * 2 * rows, up_w), (2 * dn_r, width), (n * 2 * rows, at_w), (n * 2 * rows, at_w),
         (n * 2 * rows, at_w), (2 * mx_r, width), (width,), (width,),

time: 96 us -> 74.4 us (0.78)
  local copies, waits for them, and re-layouts: 13.2 us -> 0 us
  Pallas kernels: 79.1 us -> 72.4 us
  other arithmetic: 2.56 us -> 1.2 us
    unnamed x30 -> x0, local copies, waits for them, and re-layouts: 13.2 us -> none
    pallas_call x1, Pallas kernels: 71.9 us -> 68.5 us  [fused(): pl.pallas_call(functools.partial(gather_kernel, n, nz, dims), out_shape=m...]
    pallas_call x1, Pallas kernels: 7.16 us -> 3.86 us  [fused(): pl.pallas_call(functools.partial(write_kernel, dims), out_shape=[S((n, 2,...]
    pallas_call x2, other arithmetic: 2.56 us -> 1.2 us  [fused(): pl.pallas_call(functools.partial(write_kernel, dims), out_shape=[S((n, 2,...]
where the time goes in v2:
time: 74.4 us; the launch traced here: 74.2 us
  Pallas kernels  72.4 us (97%)
  other arithmetic  1.2 us (2%)
    pallas_call x1, Pallas kernels, fused(): pl.pallas_call(functools.partial(gather_kernel, n, nz, dims), out_shape=m...  68.5 us
    pallas_call x1, Pallas kernels, fused(): pl.pallas_call(functools.partial(write_kernel, dims), out_shape=[S((n, 2,...  3.86 us

profile of v2, /device:TPU:0, one launch (start us, length us, event | category | flops | bytes accessed | tf_op | source)
XLA Modules:
  0.0 74.2 jit_solution(3911385264744238860)
XLA Ops:
  0.7 68.5 %sum_and_share.1 = (bf16[8,2,64,1792]{3,2,1,0:T(8,128)(2,1)S(1)}, bf16[8,2,640,128]{3,2,1,0:T(8,128)(2,1)S(1)}, f32[2,64,1792]{2,1,0:T(8,128)S(1)}, f32[2,640,128]{2,1,0:T(8,128)S(1)}, f32[8,2,128]{2,1,0:T(2,128)S(1)}) custom-call(f32[4,2,2,64,1024]{4,3,2,1,0:T(8,128)} %bitcast.28, f32[4,2,2,64,256]{4,3,2,1,0:T(8,128)} %bitcast.30, ...), custom_call_target="tpu_custom_call" | custom-call | tf_op jit(solution)/shard_map/sum_and_share/pallas_call | solution.py:588
  69.2 3.9 %write_out.1 = (bf16[8,2,64,1024]{3,2,1,0:T(8,128)(2,1)}, bf16[2,512,1024]{2,1,0:T(8,128)(2,1)}, bf16[8,2,64,256]{3,2,1,0:T(8,128)(2,1)}, bf16[8,2,64,256]{3,2,1...) custom-call(bf16[8,2,64,1792]{3,2,1,0:T(8,128)(2,1)S(1)} %get-tuple-, ...), custom_call_target="tpu_custom_call" | custom-call | tf_op jit(solution)/shard_map/write_out/pallas_call | solution.py:606
  73.0 0.6 reduce
  73.6 0.6 reduce.1
